TPU v7x, 128 devices: a whole 4x4x4 slice. The times are simulated.
128 devices in a mesh: dp: 8 (over z_hi, y), tensor: 16 (over z_lo, x, core).
Axes of the slice: x: 4, y: 4, z: 4 (z_hi: 2, z_lo: 2; z = z_hi * 2 + z_lo), core: 2. Of those that a mesh axis runs over, the one named last changes fastest.
Arguments:
- normed_input: bfloat16 [8192, 8192], P('dp', 'tensor'), may hold values from -6 to 6
- positions: int32 [8192], P('dp'), may hold values from 0 to 8191
- fixed_weight_matrix: bfloat16 [8192, 10240], P('dp', 'tensor'), may hold values from -0.09375 to 0.09375
- adapter_down_map: bfloat16 [8192, 16], P('tensor'), may hold values from -0.0625 to 0.0625
- adapter_up_map: bfloat16 [16, 10240], P(None, 'tensor'), may hold values from -0.0625 to 0.0625
- output_gradient: bfloat16 [8192, 10240], P('dp', 'tensor'), may hold values from -6 to 6
Outputs:
- grad_x: bfloat16 [8192, 8192], P('dp', 'tensor')
- grad_a: float32 [8192, 16], P('tensor')
- grad_b: float32 [16, 10240], P(None, 'tensor')
All inputs are finite; a program needn't handle non-finite values.
Results may differ from a plain program's by a relative error of at most 0.0048.
Values may be sent and summed in bfloat16 or wider, within the bound.
No kernel may reach another device: no remote copies, remote signals or barrier semaphores. Data moves between devices by JAX's collectives and lax.ppermute only.
A program may use at most 256 MiB of HBM per device.

v0:
```python
import math
import jax
import jax.numpy as jnp
from jax import lax
from jax.sharding import PartitionSpec as P

MODEL_WIDTH = 8192
KV = 1024
HEAD = 128


def copy_for_each(value, axis):
    peers = lax.axis_size(axis)
    return lax.all_to_all(
        jnp.broadcast_to(value[None], (peers, *value.shape)), axis, 0, 0, tiled=True
    )


def over_copies(value, axis):
    everything = copy_for_each(value, axis)
    return jnp.sum(everything, axis=0)


def together(arrays, axis):
    ends = [0]
    for a in arrays:
        ends.append(ends[-1] + a.size)
    running = over_copies(jnp.concatenate([a.ravel() for a in arrays]), axis)
    return tuple((running[b:e].reshape(a.shape) for a, b, e in zip(arrays, ends, ends[1:])))


def rope_tables(positions, width, shards, shard):
    q_width = MODEL_WIDTH // shards
    k_width = KV // shards
    offset = jnp.arange(width, dtype=jnp.int32)
    is_query = offset < q_width
    is_key = jnp.logical_and(offset >= q_width, offset < q_width + k_width)
    dimension = jnp.where(
        is_query, (shard * q_width + offset) % HEAD, (shard * k_width + offset - q_width) % HEAD
    )
    pair = (dimension // 2).astype(jnp.float32)
    freq = jnp.float32(500000.0) ** (-2.0 * pair / HEAD)
    angle = positions.astype(jnp.float32)[:, None] * freq[None, :]
    rotate = jnp.logical_or(is_query, is_key)[None, :]
    cosine = jnp.where(rotate, jnp.cos(angle), jnp.float32(1.0))
    sine = jnp.where(rotate, jnp.sin(angle), jnp.float32(0.0))
    return (cosine[:, 0::2], sine[:, 0::2])


def on_device(
    normed_input, positions, fixed_weight_matrix, adapter_down_map, adapter_up_map, output_gradient
):
    rows, width = output_gradient.shape
    shards = lax.axis_size("tensor")
    shard = lax.axis_index("tensor")
    cosine, sine = rope_tables(positions, width, shards, shard)
    pairs = output_gradient.astype(jnp.float32).reshape(rows, width // 2, 2)
    first = pairs[:, :, 0] * cosine + pairs[:, :, 1] * sine
    second = pairs[:, :, 1] * cosine - pairs[:, :, 0] * sine
    unrotated_gradient = (
        jnp.stack([first, second], axis=2).reshape(rows, width).astype(jnp.bfloat16)
    )
    rank_input = jnp.dot(normed_input, adapter_down_map, preferred_element_type=jnp.float32)
    rank_gradient = jnp.dot(
        unrotated_gradient, adapter_up_map.T, preferred_element_type=jnp.float32
    )
    rank_input, rank_gradient = together((rank_input, rank_gradient), "tensor")
    low_xb = rank_input.astype(jnp.bfloat16)
    rank_gradient_up = rank_gradient.astype(jnp.bfloat16)
    factor = 2.0 / math.sqrt(rows * lax.axis_size("dp"))
    part_a = factor * jnp.dot(normed_input.T, rank_gradient_up, preferred_element_type=jnp.float32)
    part_b = factor * jnp.dot(low_xb.T, unrotated_gradient, preferred_element_type=jnp.float32)
    terms = jnp.dot(
        unrotated_gradient,
        lax.all_gather(fixed_weight_matrix, "dp", axis=0, tiled=True).T,
        preferred_element_type=jnp.float32,
    )
    base = lax.psum_scatter(terms, "tensor", scatter_dimension=1, tiled=True)
    adapter_branch = jnp.dot(
        rank_gradient_up, adapter_down_map.T, preferred_element_type=jnp.float32
    )
    grad_x = (base + 2.0 * adapter_branch).astype(jnp.bfloat16)
    grad_a, grad_b = together((part_a, part_b), "dp")
    return (grad_x, grad_a, grad_b)


def solution(mesh):
    placed = (
        P("dp", "tensor"),
        P("dp"),
        P("dp", "tensor"),
        P("tensor", None),
        P(None, "tensor"),
        P("dp", "tensor"),
    )
    return jax.shard_map(
        on_device,
        mesh=mesh,
        in_specs=placed,
        out_specs=(P("dp", "tensor"), P("tensor", None), P(None, "tensor")),
        check_vma=False,
    )
```

profile of v0, /device:TPU:1, one launch (start us, length us, event | category | flops | bytes accessed | tf_op | source)
XLA Modules:
  0.0 383.9 jit_solution(10950872956848355848)
XLA Ops:
  7.2 0.0 copy-start
  7.2 0.0 copy-start.4
  7.2 0.0 all-gather.2.cloned.1.call-start
  7.2 0.7 all-gather.2.cloned.1.call-update
  7.9 0.0 reduce-scatter.2.cloned.1.call-start
  8.0 0.0 copy-done.4
  8.0 11.1 %fusion = (f32[1024,640]{0,1:T(8,128)}, f32[1024,640]{0,1:T(8,128)}) fusion(f32[640]{0:T(1024)S(1)} %fusion.16, f32[1024]{0:T(1024)S(1)} %convert_element_type.26, pred[640]{0:T(1024)(128)(4,1)S(1)} %fusion.10), kind=kLoop, calls=%fused_computation.2 | loop fusion | flops 1966080 | bytes 5250176 | tf_op jit(solution)/shard_map/jit(_where)/select_n | solution.py:45
  19.1 5.1 %slice.57 = f32[1024,320]{0,1:T(8,128)S(1)} slice(f32[1024,640]{0,1:T(8,128)} %get-tuple-element.19), slice={[0:1024:1], [0:640:2]} | slice | bytes 2621440 | tf_op jit(solution)/shard_map/slice | solution.py:47
  24.3 3.0 copy.22
  27.2 4.4 %reshape.138 = f32[1024,320,2]{0,2,1:T(2,128)} reshape(f32[1024,640]{0,1:T(8,128)} %copy.22) | data formatting | bytes 5242880 | tf_op jit(solution)/shard_map/reshape | solution.py:57
  31.6 6.5 %slice.55 = f32[1024,320]{0,1:T(8,128)} slice(f32[1024,640]{0,1:T(8,128)} %get-tuple-element.18), slice={[0:1024:1], [0:640:2]} | slice | bytes 2621440 | tf_op jit(solution)/shard_map/slice | solution.py:47
  38.2 0.0 copy-start.1
  38.2 4.9 %fusion.22 = (f32[1024,320,1]{0,2,1:T(1,128)S(1)}, f32[1024,320,1]{0,2,1:T(1,128)S(1)}) fusion(f32[1024,320,2]{0,2,1:T(2,128)} %reshape.138), kind=kLoop, calls=%fused_computation.48 | loop fusion | bytes 5242880 | tf_op jit(solution)/shard_map/slice | solution.py:58
  43.1 0.0 copy-done.1
  43.1 1.0 fusion.8
  44.1 0.1 pad_maximum_fusion
  44.3 2.4 copy.23
  46.7 3.2 convert_element_type.28
  49.9 90.7 %all-gather.2.cloned.1.call-done = bf16[8192,640]{1,0:T(8,128)(2,1)} async-done(((bf16[1024,640]{1,0:T(8,128)(2,1)}), bf16[8192,640]{1,0:T(8,128)(2,1)}) %all-gather.2.cloned.1.call-update) | async-done | bytes 10485776 | tf_op jit(solution)/shard_map/all_gather | solution.py:75
  140.6 21.2 %fusion.24 = f32[1024,8192]{1,0:T(8,128)} fusion(bf16[1024,640]{0,1:T(8,128)(2,1)S(1)} %convert_element_type.28, bf16[8192,640]{1,0:T(8,128)(2,1)} %all-gather.2.cloned.1.call-done), kind=kOutput, calls=%fused_computation.50 | convolution fusion | flops 10737418240 | bytes 45350912 | tf_op jit(solution)/shard_map/dot_general | solution.py:73
  161.8 0.0 copy-start.3
  161.8 0.0 reduce-scatter.2.cloned.1.call-update
  161.8 0.7 copy-done.3
  162.5 0.0 copy-start.2
  162.5 0.6 fusion.26
  163.1 0.2 reshape.133
  163.3 0.0 copy-done
  163.3 0.0 copy-done.2
  163.3 0.4 fusion.25
  163.7 0.2 reshape.132
  163.9 1.6 broadcast_in_dim.38
  165.5 44.0 %all_to_all.12 = f32[16,1,32768]{2,1,0:T(1,128)} all-to-all(f32[16,1,32768]{2,1,0:T(1,128)S(1)} %broadcast_in_dim.38), channel_id=1, replica_groups=mesh['dp'=8,'tensor'=16] {'tensor'}, dimensions={0} | all-to-all | bytes 4194304 | tf_op jit(solution)/shard_map/all_to_all | solution.py:14
  209.5 3.0 reduce_sum.18
  212.5 0.2 convert_element_type.29
  212.7 0.2 convert_element_type.31
  212.9 0.4 convolution_multiply_fusion
  213.4 0.3 fusion.6
  213.6 0.1 copy.27
  213.8 0.1 reshape.134
  213.9 0.3 broadcast_in_dim.39
  214.3 157.9 %all_to_all.13 = f32[8,1,18432]{2,1,0:T(1,128)S(1)} all-to-all(f32[8,1,18432]{2,1,0:T(1,128)S(1)} %broadcast_in_dim.39), channel_id=1, replica_groups=mesh['dp'=8,'tensor'=16] {'dp'}, dimensions={0} | all-to-all | bytes 1179648 | tf_op jit(solution)/shard_map/all_to_all | solution.py:14
  372.2 0.4 reduce_sum.19
  372.7 0.1 slice.61
  372.8 0.7 copy.29
  373.5 0.6 reshape.136
  374.1 0.0 reduce-scatter.2.cloned.1.call-done
  374.1 3.0 add_convert_fusion
  (9 shorter events, 0.1 us)
Async XLA Ops:
  7.2 156.1 %copy-start = (bf16[1024,512]{1,0:T(8,128)(2,1)S(1)}, bf16[1024,512]{1,0:T(8,128)(2,1)}, u32[]{:S(2)}) copy-start(bf16[1024,512]{1,0:T(8,128)(2,1)} %param.6) | copy-start | bytes 3145732
  7.2 0.8 copy-start.4
  7.2 133.4 %all-gather.2.cloned.1.call-start = ((), (), s32[]{:S(2)}) async-start(), calls=%async_computation.3 | async-start | bytes 11796480 | tf_op jit(solution)/shard_map/all_gather | solution.py:75
  7.9 366.2 %reduce-scatter.2.cloned.1.call-start = ((), (), s32[]{:S(2)}) async-start(), calls=%async_computation.4 | async-start | bytes 35651584 | tf_op jit(solution)/shard_map/reduce_scatter | solution.py:78
  38.2 4.9 %copy-start.1 = (f32[1024,320]{0,1:T(8,128)S(1)}, f32[1024,320]{0,1:T(8,128)}, u32[]{:S(2)}) copy-start(f32[1024,320]{0,1:T(8,128)} %slice.55) | copy-start | bytes 3932164
  161.8 0.7 copy-start.3
  162.5 0.8 copy-start.2
Sparse Core Ops, SparseCore 0:
  10.3 130.2 all-gather.1
  161.9 204.8 reduce-scatter.1
where the time goes:
time: 385 us; the launch traced here: 384 us
  blocking collectives  202 us (52%)
  waiting for transfers between devices  91.4 us (24%)
  local copies, waits for them, and re-layouts  34.8 us (9%)
  matrix products  25.8 us (7%)
  other arithmetic  15.7 us (4%)
  between operations  14.3 us (4%)
    all_to_all x2, blocking collectives, copy_for_each(): lax.all_to_all(jnp.broadcast_to(value[None], (peers, *value.shape)), axis...  202 us
    all_gather x1, waiting for transfers between devices, on_device(): lax.all_gather(fixed_weight_matrix, 'dp', axis=0, tiled=True)  90.7 us
    dot_general x1, matrix products, on_device(): jnp.dot(unrotated_gradient, lax.all_gather(fixed_weight_matrix, 'dp', axi...  21.2 us
    slice x2, local copies, waits for them, and re-layouts, rope_tables(): return (cosine[:, 0::2], sine[:, 0::2])  11.7 us
    select_n x1, other arithmetic, rope_tables(): cosine = jnp.where(rotate, jnp.cos(angle), jnp.float32(1.0))  11.1 us
  transfers between devices with their start and end apart: 2, of which 1 were waited for; matrix products, arithmetic and copies ran while one was open for 13% of the time, Pallas kernels for 0%

commit v1 on v0

--- a/solution.py
+++ b/solution.py
@@ -70,9 +70,13 @@
     factor = 2.0 / math.sqrt(rows * lax.axis_size("dp"))
     part_a = factor * jnp.dot(normed_input.T, rank_gradient_up, preferred_element_type=jnp.float32)
     part_b = factor * jnp.dot(low_xb.T, unrotated_gradient, preferred_element_type=jnp.float32)
+    order_members_all = lambda buf, array_axis: jnp.concatenate(
+        jax.lax.all_to_all(jnp.stack([buf for _ in range(jax.lax.axis_size("dp"))], 0), "dp", 0, 0),
+        array_axis,
+    )
     terms = jnp.dot(
         unrotated_gradient,
-        lax.all_gather(fixed_weight_matrix, "dp", axis=0, tiled=True).T,
+        order_members_all(fixed_weight_matrix, 0).T,
         preferred_element_type=jnp.float32,
     )
     base = lax.psum_scatter(terms, "tensor", scatter_dimension=1, tiled=True)

time: 385 us -> 424 us (1.10)
  the two profiles are of different devices: /device:TPU:1 before, /device:TPU:25 now
where the time goes in v1:
time: 424 us; the launch traced here: 423 us
  blocking collectives  206 us (49%)
  waiting for transfers between devices  113 us (27%)
  local copies, waits for them, and re-layouts  40.8 us (10%)
  matrix products  25.8 us (6%)
  other arithmetic  15.7 us (4%)
  between operations  14.2 us (3%)
  starting transfers between devices  7.58 us (2%)
    all_to_all x2, blocking collectives, copy_for_each(): lax.all_to_all(jnp.broadcast_to(value[None], (peers, *value.shape)), axis...  206 us
    all_to_all x1, waiting for transfers between devices, on_device(): jax.lax.all_to_all(jnp.stack([buf for _ in range(jax.lax.axis_size('dp'))...  113 us
    dot_general x1, matrix products, on_device(): jnp.dot(unrotated_gradient, order_members_all(fixed_weight_matrix, 0).T,...  21.2 us
    slice x2, local copies, waits for them, and re-layouts, rope_tables(): return (cosine[:, 0::2], sine[:, 0::2])  11.6 us
    select_n x1, other arithmetic, rope_tables(): sine = jnp.where(rotate, jnp.sin(angle), jnp.float32(0.0))  11.1 us
  transfers between devices with their start and end apart: 2, of which 1 were waited for; matrix products, arithmetic and copies ran while one was open for 12% of the time, Pallas kernels for 0%

profile of v1, /device:TPU:25, one launch (start us, length us, event | category | flops | bytes accessed | tf_op | source)
XLA Modules:
  0.0 423.0 jit_solution(10203084942013119209)
XLA Ops:
  7.2 0.0 copy-start
  7.2 6.2 %stack.11 = bf16[8,1024,640]{2,1,0:T(8,128)(2,1)} broadcast(bf16[1024,640]{1,0:T(8,128)(2,1)} %param.8), dimensions={1,2} | broadcast | bytes 11796480 | tf_op jit(solution)/shard_map/stack | solution.py:74
  13.4 0.0 copy-start.4
  13.4 7.6 %all-to-all-start = ((bf16[8,1024,640]{2,1,0:T(8,128)(2,1)}), bf16[8,1024,640]{2,1,0:T(8,128)(2,1)}, u32[]{:S(2)}, u32[]{:S(2)}) async-start(bf16[8,1024,640]{2,1,0:T(8,128)(2,1)} %stack.11), calls=%async_computation | async-start | bytes 20971520 | tf_op jit(solution)/shard_map/all_to_all | solution.py:74
  20.9 0.0 reduce-scatter.2.cloned.1.call-start
  21.0 0.0 copy-done.4
  21.0 11.1 %fusion.1 = (f32[1024,640]{0,1:T(8,128)}, f32[1024,640]{0,1:T(8,128)}) fusion(f32[640]{0:T(1024)S(1)} %fusion.14, f32[1024]{0:T(1024)S(1)} %convert_element_type.35, pred[640]{0:T(1024)(128)(4,1)S(1)} %fusion.8), kind=kLoop, calls=%fused_computation.3 | loop fusion | flops 1966080 | bytes 5250176 | tf_op jit(solution)/shard_map/jit(_where)/select_n | solution.py:46
  32.1 5.1 %slice.57 = f32[1024,320]{0,1:T(8,128)S(1)} slice(f32[1024,640]{0,1:T(8,128)} %get-tuple-element.18), slice={[0:1024:1], [0:640:2]} | slice | bytes 2621440 | tf_op jit(solution)/shard_map/slice | solution.py:47
  37.1 6.5 %slice.55 = f32[1024,320]{0,1:T(8,128)} slice(f32[1024,640]{0,1:T(8,128)} %get-tuple-element.19), slice={[0:1024:1], [0:640:2]} | slice | bytes 2621440 | tf_op jit(solution)/shard_map/slice | solution.py:47
  43.7 2.9 copy.22
  46.6 4.4 %reshape.151 = f32[1024,320,2]{0,2,1:T(2,128)} reshape(f32[1024,640]{0,1:T(8,128)} %copy.22) | data formatting | bytes 5242880 | tf_op jit(solution)/shard_map/reshape | solution.py:57
  51.0 0.0 copy-start.1
  51.0 4.9 %fusion.20 = (f32[1024,320,1]{0,2,1:T(1,128)S(1)}, f32[1024,320,1]{0,2,1:T(1,128)S(1)}) fusion(f32[1024,320,2]{0,2,1:T(2,128)} %reshape.151), kind=kLoop, calls=%fused_computation.46 | loop fusion | bytes 5242880 | tf_op jit(solution)/shard_map/slice | solution.py:58
  55.9 0.0 copy-done.1
  55.9 1.0 fusion.3
  56.9 0.1 maximum_convert_fusion
  57.1 2.4 copy.23
  59.5 3.2 convert_element_type.38
  62.7 113.2 %all-to-all-done = bf16[8,1024,640]{2,1,0:T(8,128)(2,1)} async-done(((bf16[8,1024,640]{2,1,0:T(8,128)(2,1)}), bf16[8,1024,640]{2,1,0:T(8,128)(2,1)}, u32[]{:S(2)}, u32[]{:S(2)}) %all-to-all-start) | async-done | bytes 10485792 | tf_op jit(solution)/shard_map/all_to_all | solution.py:74
  175.8 21.2 %fusion.22 = f32[1024,8192]{1,0:T(8,128)} fusion(bf16[1024,640]{0,1:T(8,128)(2,1)S(1)} %convert_element_type.38, bf16[8192,640]{1,0:T(8,128)(2,1)} %bitcast.2), kind=kOutput, calls=%fused_computation.48 | convolution fusion | flops 10737418240 | bytes 45350912 | tf_op jit(solution)/shard_map/dot_general | solution.py:77
  197.0 0.0 copy-start.3
  197.0 0.0 reduce-scatter.2.cloned.1.call-update
  197.1 0.7 copy-done.3
  197.8 0.0 copy-start.2
  197.8 0.6 fusion.24
  198.3 0.2 reshape.146
  198.5 0.0 copy-done
  198.5 0.0 copy-done.2
  198.5 0.4 fusion.23
  198.9 0.2 reshape.145
  199.2 1.6 broadcast_in_dim.38
  200.8 43.9 %all_to_all.17 = f32[16,1,32768]{2,1,0:T(1,128)} all-to-all(f32[16,1,32768]{2,1,0:T(1,128)S(1)} %broadcast_in_dim.38), channel_id=1, replica_groups=mesh['dp'=8,'tensor'=16] {'tensor'}, dimensions={0} | all-to-all | bytes 4194304 | tf_op jit(solution)/shard_map/all_to_all | solution.py:14
  244.7 3.0 reduce_sum.18
  247.7 0.2 convert_element_type.39
  247.9 0.2 convert_element_type.41
  248.1 0.4 convolution_multiply_fusion
  248.6 0.3 fusion.6
  248.8 0.1 copy.27
  249.0 0.1 reshape.147
  249.1 0.3 broadcast_in_dim.39
  249.4 161.8 %all_to_all.18 = f32[8,1,18432]{2,1,0:T(1,128)S(1)} all-to-all(f32[8,1,18432]{2,1,0:T(1,128)S(1)} %broadcast_in_dim.39), channel_id=1, replica_groups=mesh['dp'=8,'tensor'=16] {'dp'}, dimensions={0} | all-to-all | bytes 1179648 | tf_op jit(solution)/shard_map/all_to_all | solution.py:14
  411.3 0.4 reduce_sum.19
  411.7 0.1 slice.61
  411.9 0.7 copy.29
  412.6 0.6 reshape.149
  413.2 0.0 reduce-scatter.2.cloned.1.call-done
  413.2 3.0 add_convert_fusion
  (9 shorter events, 0.1 us)
Async XLA Ops:
  7.2 191.4 %copy-start = (bf16[1024,512]{1,0:T(8,128)(2,1)S(1)}, bf16[1024,512]{1,0:T(8,128)(2,1)}, u32[]{:S(2)}) copy-start(bf16[1024,512]{1,0:T(8,128)(2,1)} %param.6) | copy-start | bytes 3145732
  13.4 7.6 %copy-start.4 = (s32[1024]{0:T(1024)S(1)}, s32[1024]{0:T(1024)}, u32[]{:S(2)}) copy-start(s32[1024]{0:T(1024)} %param.7) | copy-start | bytes 12292
  13.4 162.5 %all-to-all-start = ((bf16[8,1024,640]{2,1,0:T(8,128)(2,1)}), bf16[8,1024,640]{2,1,0:T(8,128)(2,1)}, u32[]{:S(2)}, u32[]{:S(2)}) async-start(bf16[8,1024,640]{2,1,0:T(8,128)(2,1)} %stack.11), calls=%async_computation | async-start | bytes 20971520 | tf_op jit(solution)/shard_map/all_to_all | solution.py:74
  20.9 392.3 %reduce-scatter.2.cloned.1.call-start = ((), (), s32[]{:S(2)}) async-start(), calls=%async_computation.4 | async-start | bytes 35651584 | tf_op jit(solution)/shard_map/reduce_scatter | solution.py:82
  51.0 4.9 %copy-start.1 = (f32[1024,320]{0,1:T(8,128)S(1)}, f32[1024,320]{0,1:T(8,128)}, u32[]{:S(2)}) copy-start(f32[1024,320]{0,1:T(8,128)} %slice.55) | copy-start | bytes 3932164
  197.0 0.7 copy-start.3
  197.8 0.8 copy-start.2
Sparse Core Ops, SparseCore 0:
  197.2 208.3 reduce-scatter.1
